TPU v7x, 32 devices: a whole 2x2x4 slice. The times are simulated.
32 devices in a mesh: dp: 2 (over x), lat: 4 (over y, core), lon: 4 (over z).
Axes of the slice: x: 2, y: 2, z: 4, core: 2. Of those that a mesh axis runs over, the one named last changes fastest.
Arguments:
- hidden_in: bfloat16 [2, 64, 512, 128], P('dp', 'lat', 'lon'), may hold values from -6 to 6
- conv_weight: bfloat16 [3, 3, 128, 128], replicated, may hold values from -0.1875 to 0.1875
- conv_bias: float32 [128], replicated, may hold values from -3 to 3
- proj_weight: float32 [128], replicated, may hold values from -5 to 5
- ocean_depth: float32 [64, 512], P('lat', 'lon'), may hold values from 0.5 to 2
- sea_mask: int32 [64, 512], P('lat', 'lon'), may hold values 0 or 1
- step_alpha: float32 [6], replicated, may hold values from 0.04 to 0.07
- step_beta: float32 [6], replicated, may hold values from 0.1 to 0.5
- surface_cotangent: float32 [2, 64, 512], P('dp', 'lat', 'lon'), may hold values from -20 to 20
Outputs:
- grad_hidden: bfloat16 [2, 64, 512, 128], P('dp', 'lat', 'lon')
- grad_weight: float32 [128, 3, 3, 128], P(('lat', 'lon'))
- grad_bias: float32 [128], replicated
- grad_proj: float32 [128], replicated
All inputs are finite; a program needn't handle non-finite values. No bound on the sum of `sea_mask` on one device may be relied on, other than what follows from the above.
Results may differ from a plain program's by a relative error of at most 0.01.
Values may be sent and summed in bfloat16 or wider, within the bound.
A program may use at most 64 MiB of HBM per device.

v0:
```python
import math
import jax
import jax.numpy as jnp
from jax import lax
from jax.sharding import PartitionSpec as P

ITERS = 6
helm_coef = 0.5


def extended(cells, sides, width, closed):
    for axis, dim in sides:
        count = lax.axis_size(axis)
        ends = count if closed else count - 1
        head = lax.slice_in_dim(cells, 0, width, axis=dim)
        tail = lax.slice_in_dim(cells, cells.shape[dim] - width, cells.shape[dim], axis=dim)
        cells = jnp.concatenate(
            [
                lax.ppermute(tail, axis, [(i, (i + 1) % count) for i in range(ends)]),
                cells,
                lax.ppermute(head, axis, [((i + 1) % count, i) for i in range(ends)]),
            ],
            axis=dim,
        )
    return cells


def operate(field_ext, mask_ext, depth_ext):
    rows_in = field_ext.shape[-2] - 2
    cols_in = field_ext.shape[-1] - 2
    center = field_ext[..., 1:-1, 1:-1]
    mask_mid = mask_ext[1:-1, 1:-1]
    depth_mid = depth_ext[1:-1, 1:-1]
    result = helm_coef * center
    for row_off, col_off in ((0, 1), (2, 1), (1, 0), (1, 2)):
        beside = field_ext[..., row_off : row_off + rows_in, col_off : col_off + cols_in]
        mask_near = mask_ext[row_off : row_off + rows_in, col_off : col_off + cols_in]
        depth_near = depth_ext[row_off : row_off + rows_in, col_off : col_off + cols_in]
        weight = mask_near * 0.5 * (depth_mid + depth_near)
        result = result + weight * (center - beside)
    return mask_mid * result


def solve_steps(adjoint_start, mask_ext, depth_ext, step_alpha, step_beta, widen):
    solution = jnp.zeros_like(adjoint_start)
    residual = adjoint_start
    direction = adjoint_start
    for turn_index in range(ITERS):
        solution = solution + step_alpha[turn_index] * direction
        if turn_index + 1 < ITERS:
            applied = operate(widen(direction), mask_ext, depth_ext)
            residual = residual - step_alpha[turn_index] * applied
            direction = residual + step_beta[turn_index] * direction
    return solution


def halo_field(field):
    field = extended(field, (("lat", 1),), 1, False)
    return extended(field, (("lon", 2),), 1, True)


def shards(
    hidden_in,
    conv_weight,
    conv_bias,
    proj_weight,
    ocean_depth,
    sea_mask,
    step_alpha,
    step_beta,
    surface_cotangent,
):
    samples, lat_rows, lon_cols, channels = hidden_in.shape
    mask_float = sea_mask.astype(jnp.float32)
    counted, summed = lax.psum(
        (jnp.sum(mask_float), jnp.sum(mask_float * surface_cotangent, axis=(1, 2))), ("lat", "lon")
    )
    adjoint_start = mask_float * (surface_cotangent - (summed / counted)[:, None, None])
    coefs = jnp.stack([mask_float, ocean_depth])
    coefs = extended(coefs, (("lat", 1),), 1, False)
    coefs = extended(coefs, (("lon", 2),), 1, True)
    solution = solve_steps(adjoint_start, coefs[0], coefs[1], step_alpha, step_beta, halo_field)
    forcing_grad = mask_float * solution
    padded = extended(hidden_in, (("lat", 1),), 1, False)
    padded = extended(padded, (("lon", 2),), 1, True)
    cell_count = samples * lat_rows * lon_cols
    shifted = [
        padded[:, row_off : row_off + lat_rows, col_off : col_off + lon_cols, :].reshape(
            cell_count, channels
        )
        for row_off in range(3)
        for col_off in range(3)
    ]
    preact = conv_bias
    for offset in range(9):
        preact = preact + jnp.dot(
            shifted[offset],
            conv_weight[offset // 3, offset % 3],
            preferred_element_type=jnp.float32,
        )
    sigma = jax.nn.sigmoid(preact)
    active = preact * sigma
    slope_act = sigma * (1.0 + preact * (1.0 - sigma))
    force_col = forcing_grad.reshape(cell_count)[:, None]
    grad_pre = (force_col * proj_weight * slope_act).astype(jnp.bfloat16)
    local_proj = jnp.sum(active * force_col, axis=0)
    local_bias = jnp.sum(grad_pre.astype(jnp.float32), axis=0)
    grad_ext = extended(
        grad_pre.reshape(samples, lat_rows, lon_cols, channels), (("lat", 1),), 1, False
    )
    grad_ext = extended(grad_ext, (("lon", 2),), 1, True)
    backed = jnp.zeros((cell_count, channels), jnp.float32)
    for row_off in range(3):
        for col_off in range(3):
            window = grad_ext[
                :, 2 - row_off : 2 - row_off + lat_rows, 2 - col_off : 2 - col_off + lon_cols, :
            ].reshape(cell_count, channels)
            backed = backed + lax.dot_general(
                window,
                conv_weight[row_off, col_off],
                (((1,), (1,)), ((), ())),
                preferred_element_type=jnp.float32,
            )
    grad_hidden = backed.reshape(samples, lat_rows, lon_cols, channels).astype(jnp.bfloat16)
    share = channels // lax.axis_size(("lat", "lon"))
    blocks = []
    for shifted_cols in shifted:
        blocks.append(
            lax.dot_general(
                shifted_cols, grad_pre, (((0,), (0,)), ((), ())), preferred_element_type=jnp.float32
            )
        )
    spatial = lax.psum_scatter(
        jnp.stack(blocks, axis=1).reshape(share * lax.axis_size(("lat", "lon")), 3, 3, channels),
        ("lat", "lon"),
        scatter_dimension=0,
        tiled=True,
    )
    own_weight = lax.psum(spatial, "dp")
    total_bias, total_proj = lax.psum((local_bias, local_proj), ("dp", "lat", "lon"))
    all_cells = cell_count * lax.axis_size("dp") * lax.axis_size("lat") * lax.axis_size("lon")
    grad_scale = 1.0 / math.sqrt(all_cells)
    return (grad_hidden, own_weight * grad_scale, total_bias * grad_scale, total_proj * grad_scale)


def solution(mesh):
    in_specs = (
        P("dp", "lat", "lon", None),
        P(),
        P(),
        P(),
        P("lat", "lon"),
        P("lat", "lon"),
        P(),
        P(),
        P("dp", "lat", "lon"),
    )
    out_specs = (P("dp", "lat", "lon", None), P(("lat", "lon"), None, None, None), P(), P())
    return jax.shard_map(shards, mesh=mesh, in_specs=in_specs, out_specs=out_specs, check_vma=False)
```

profile of v0, /device:TPU:0, one launch (start us, length us, event | category | flops | bytes accessed | tf_op | source)
XLA Modules:
  0.0 225.2 jit_solution(6670252528962750081)
XLA Ops:
  8.7 2.4 %collective-permute-start = (f32[2,1,128]{2,1,0:T(1,128)S(1)}, f32[2,1,128]{2,1,0:T(1,128)S(1)}, u32[]{:S(2)}, u32[]{:S(2)}) collective-permute-start(f32[2,1,128]{2,1,0:T(1,128)S(1)} %get-tuple-element.57), channel_id=1, source_target_pairs={{0,4},{4,8},{8,12},{1,5},{5,9},{9,13},{2,6},{6,10},{10,14},{3,7},{... | collective-permute-start | bytes 3080 | tf_op jit(solution)/shard_map/ppermute | solution.py:19
  15.0 36.6 %all-reduce.1 = (f32[1]{0:T(128)}, f32[1]{0:T(128)}) all-reduce(f32[1]{0:T(128)} %bitcast.2, f32[1]{0:T(128)} %bitcast.3), channel_id=1, replica_groups=mesh['dp'=2,'lat'=4,'lon'=4] {'lat','lon'}, use_global_device_ids=true, to_apply=%region_1.0 | all-reduce | flops 2 | bytes 16 | tf_op jit(solution)/shard_map/psum | solution.py:75
  61.0 3.7 %collective-permute-start.3 = (f32[2,18,1]{2,1,0:T(8,128)S(1)}, f32[2,18,1]{2,1,0:T(8,128)S(1)}, u32[]{:S(2)}, u32[]{:S(2)}) collective-permute-start(f32[2,18,1]{2,1,0:T(8,128)S(1)} %get-tuple-element.56), channel_id=1, source_target_pairs={{1,0},{2,1},{3,2},{0,3},{5,4},{6,5},{7,6},{4,7},{9,8},{10,9},{11,1... | collective-permute-start | bytes 440 | tf_op jit(solution)/shard_map/ppermute | solution.py:21
  64.7 2.0 collective-permute-start.7
  69.7 2.6 %collective-permute-start.8 = (f32[1,1,128]{2,1,0:T(1,128)S(1)}, f32[1,1,128]{2,1,0:T(1,128)S(1)}, u32[]{:S(2)}, u32[]{:S(2)}) collective-permute-start(f32[1,1,128]{2,1,0:T(1,128)S(1)} %get-tuple-element.75), channel_id=1, source_target_pairs={{0,4},{4,8},{8,12},{1,5},{5,9},{9,13},{2,6},{6,10},{10,14},{3,7},{... | collective-permute-start | bytes 1544 | tf_op jit(solution)/shard_map/ppermute | solution.py:19
  73.6 4.7 %collective-permute-done.9 = f32[1,1,128]{2,1,0:T(1,128)S(1)} collective-permute-done((f32[1,1,128]{2,1,0:T(1,128)S(1)}, f32[1,1,128]{2,1,0:T(1,128)S(1)}, u32[]{:S(2)}, u32[]{:S(2)}) %collective-permute-start.9) | collective-permute-done | bytes 544 | tf_op jit(solution)/shard_map/ppermute | solution.py:21
  78.4 3.8 %collective-permute-start.11 = (f32[1,18,1]{2,1,0:T(8,128)S(1)}, f32[1,18,1]{2,1,0:T(8,128)S(1)}, u32[]{:S(2)}, u32[]{:S(2)}) collective-permute-start(f32[1,18,1]{2,1,0:T(8,128)S(1)} %get-tuple-element.66), channel_id=1, source_target_pairs={{1,0},{2,1},{3,2},{0,3},{5,4},{6,5},{7,6},{4,7},{9,8},{10,9},{11,1... | collective-permute-start | bytes 224 | tf_op jit(solution)/shard_map/ppermute | solution.py:21
  82.2 1.7 collective-permute-done.10
  85.2 3.3 %collective-permute-start.12 = (f32[1,1,128]{2,1,0:T(1,128)S(1)}, f32[1,1,128]{2,1,0:T(1,128)S(1)}, u32[]{:S(2)}, u32[]{:S(2)}) collective-permute-start(f32[1,1,128]{2,1,0:T(1,128)S(1)} %get-tuple-element.73), channel_id=1, source_target_pairs={{0,4},{4,8},{8,12},{1,5},{5,9},{9,13},{2,6},{6,10},{10,14},{3,7},{... | collective-permute-start | bytes 1544 | tf_op jit(solution)/shard_map/ppermute | solution.py:19
  89.9 2.2 collective-permute-done.13
  93.3 2.8 %collective-permute-start.15 = (f32[1,18,1]{2,1,0:T(8,128)S(1)}, f32[1,18,1]{2,1,0:T(8,128)S(1)}, u32[]{:S(2)}, u32[]{:S(2)}) collective-permute-start(f32[1,18,1]{2,1,0:T(8,128)S(1)} %get-tuple-element.64), channel_id=1, source_target_pairs={{1,0},{2,1},{3,2},{0,3},{5,4},{6,5},{7,6},{4,7},{9,8},{10,9},{11,1... | collective-permute-start | bytes 224 | tf_op jit(solution)/shard_map/ppermute | solution.py:21
  99.0 3.4 %collective-permute-start.16 = (f32[1,1,128]{2,1,0:T(1,128)S(1)}, f32[1,1,128]{2,1,0:T(1,128)S(1)}, u32[]{:S(2)}, u32[]{:S(2)}) collective-permute-start(f32[1,1,128]{2,1,0:T(1,128)S(1)} %get-tuple-element.71), channel_id=1, source_target_pairs={{0,4},{4,8},{8,12},{1,5},{5,9},{9,13},{2,6},{6,10},{10,14},{3,7},{... | collective-permute-start | bytes 1544 | tf_op jit(solution)/shard_map/ppermute | solution.py:19
  103.7 2.2 collective-permute-done.17
  107.3 2.6 %collective-permute-start.19 = (f32[1,18,1]{2,1,0:T(8,128)S(1)}, f32[1,18,1]{2,1,0:T(8,128)S(1)}, u32[]{:S(2)}, u32[]{:S(2)}) collective-permute-start(f32[1,18,1]{2,1,0:T(8,128)S(1)} %get-tuple-element.62), channel_id=1, source_target_pairs={{1,0},{2,1},{3,2},{0,3},{5,4},{6,5},{7,6},{4,7},{9,8},{10,9},{11,1... | collective-permute-start | bytes 224 | tf_op jit(solution)/shard_map/ppermute | solution.py:21
  112.8 3.4 %collective-permute-start.20 = (f32[1,1,128]{2,1,0:T(1,128)S(1)}, f32[1,1,128]{2,1,0:T(1,128)S(1)}, u32[]{:S(2)}, u32[]{:S(2)}) collective-permute-start(f32[1,1,128]{2,1,0:T(1,128)S(1)} %get-tuple-element.69), channel_id=1, source_target_pairs={{0,4},{4,8},{8,12},{1,5},{5,9},{9,13},{2,6},{6,10},{10,14},{3,7},{... | collective-permute-start | bytes 1544 | tf_op jit(solution)/shard_map/ppermute | solution.py:19
  117.5 3.5 %collective-permute-start.24 = (bf16[1,1,128,128]{3,2,1,0:T(8,128)(2,1)S(1)}, bf16[1,1,128,128]{3,2,1,0:T(8,128)(2,1)S(1)}, u32[]{:S(2)}, u32[]{:S(2)}) collective-permute-start(bf16[1,1,128,128]{3,2,1,0:T(8,128)(2,1)S(1)} %get-tuple-element.52), channel_id=1, source_target_pairs={{0,4},{4,8},{8,12},{1,5},{5,9},{9,13},{2,6},{6,10},{10,14},{3,7},{... | collective-permute-start | bytes 98312 | tf_op jit(solution)/shard_map/ppermute | solution.py:19
  123.7 2.6 %collective-permute-start.23 = (f32[1,18,1]{2,1,0:T(8,128)S(1)}, f32[1,18,1]{2,1,0:T(8,128)S(1)}, u32[]{:S(2)}, u32[]{:S(2)}) collective-permute-start(f32[1,18,1]{2,1,0:T(8,128)S(1)} %get-tuple-element.60), channel_id=1, source_target_pairs={{1,0},{2,1},{3,2},{0,3},{5,4},{6,5},{7,6},{4,7},{9,8},{10,9},{11,1... | collective-permute-start | bytes 224 | tf_op jit(solution)/shard_map/ppermute | solution.py:21
  128.0 4.5 %fusion.69 = f32[2048]{0:T(1024)S(1)} fusion(f32[1,16,128]{2,1,0:T(8,128)S(1)} %get-tuple-element.11, f32[1,16,128]{2,1,0:T(8,128)S(1)} %get-tuple-element.21, f32[1,16,128]{2,1,0:T(8,128)S(1)} %get-tuple-element.10, f32[1,18,1]{2,1,0:T(8,128)S(1)} %collective-permute-done.23, f32[1,1,128]{2,1,0:T(1,128)S(1)} %collective-permute-done.21, ...), kind=kLoop, calls=%fused_computation.128 | loop fusion | flops 79872 | bytes 107692 | tf_op jit(solution)/shard_map/mul | solution.py:105
  134.2 2.6 %collective-permute-start.27 = (bf16[1,18,1,128]{3,2,1,0:T(2,128)(2,1)S(1)}, bf16[1,18,1,128]{3,2,1,0:T(2,128)(2,1)S(1)}, u32[]{:S(2)}, u32[]{:S(2)}) collective-permute-start(bf16[1,18,1,128]{3,2,1,0:T(2,128)(2,1)S(1)} %get-tuple-element.43), channel_id=1, source_target_pairs={{1,0},{2,1},{3,2},{0,3},{5,4},{6,5},{7,6},{4,7},{9,8},{10,9},{11,1... | collective-permute-start | bytes 13832 | tf_op jit(solution)/shard_map/ppermute | solution.py:21
  146.9 2.2 collective-permute-start.28
  150.4 45.0 %all-reduce = (f32[128]{0:T(128)S(1)}, f32[128]{0:T(128)S(1)}) all-reduce(f32[128]{0:T(128)S(1)} %get-tuple-element.8, f32[128]{0:T(128)S(1)} %get-tuple-element.22), channel_id=1, replica_groups=mesh['dp'=2,'lat'=4,'lon'=4] {'dp','lat','lon'}, use_global_device_ids=true, to_apply=%region_7.0 | all-reduce | flops 256 | bytes 2048 | tf_op jit(solution)/shard_map/psum | solution.py:140
  196.0 2.4 %collective-permute-start.30 = (bf16[1,18,1,128]{3,2,1,0:T(2,128)(2,1)S(1)}, bf16[1,18,1,128]{3,2,1,0:T(2,128)(2,1)S(1)}, u32[]{:S(2)}, u32[]{:S(2)}) collective-permute-start(bf16[1,18,1,128]{3,2,1,0:T(2,128)(2,1)S(1)} %get-tuple-element.37), channel_id=1, source_target_pairs={{1,0},{2,1},{3,2},{0,3},{5,4},{6,5},{7,6},{4,7},{9,8},{10,9},{11,1... | collective-permute-start | bytes 13832 | tf_op jit(solution)/shard_map/ppermute | solution.py:21
  199.7 4.1 %collective-permute-done.31 = bf16[1,18,1,128]{3,2,1,0:T(2,128)(2,1)S(1)} collective-permute-done((bf16[1,18,1,128]{3,2,1,0:T(2,128)(2,1)S(1)}, bf16[1,18,1,128]{3,2,1,0:T(2,128)(2,1)S(1)}, u32[]{:S(2)}, u32[]{:S(2)}) %collective-permute-start.31) | collective-permute-done | bytes 4640 | tf_op jit(solution)/shard_map/ppermute | solution.py:19
  207.9 9.9 %psum.37 = f32[8,3,3,128]{3,0,2,1:T(8,128)S(1)} all-reduce(f32[8,3,3,128]{3,0,2,1:T(8,128)} %reduce-scatter.2.cloned.1.call-done), channel_id=1, replica_groups=mesh['dp'=2,'lat'=4,'lon'=4] {'dp'}, use_global_device_ids=true, to_apply=%region_5.0 | all-reduce | flops 9216 | bytes 73728 | tf_op jit(solution)/shard_map/psum | solution.py:139
  (129 shorter events, 55.3 us)
Async XLA Ops:
  7.2 200.7 %reduce-scatter.2.cloned.1.call-start = ((), (), s32[]{:S(2)}) async-start(), calls=%async_computation.1 | async-start | bytes 626688 | tf_op jit(solution)/shard_map/reduce_scatter | solution.py:133
  8.7 51.3 %collective-permute-start = (f32[2,1,128]{2,1,0:T(1,128)S(1)}, f32[2,1,128]{2,1,0:T(1,128)S(1)}, u32[]{:S(2)}, u32[]{:S(2)}) collective-permute-start(f32[2,1,128]{2,1,0:T(1,128)S(1)} %get-tuple-element.57), channel_id=1, source_target_pairs={{0,4},{4,8},{8,12},{1,5},{5,9},{9,13},{2,6},{6,10},{10,14},{3,7},{... | collective-permute-start | bytes 3080 | tf_op jit(solution)/shard_map/ppermute | solution.py:19
  11.1 49.0 %collective-permute-start.1 = (f32[2,1,128]{2,1,0:T(1,128)S(1)}, f32[2,1,128]{2,1,0:T(1,128)S(1)}, u32[]{:S(2)}, u32[]{:S(2)}) collective-permute-start(f32[2,1,128]{2,1,0:T(1,128)S(1)} %get-tuple-element.58), channel_id=1, source_target_pairs={{4,0},{8,4},{12,8},{5,1},{9,5},{13,9},{6,2},{10,6},{14,10},{7,3},{... | collective-permute-start | bytes 3080 | tf_op jit(solution)/shard_map/ppermute | solution.py:21
  53.6 5.6 %collective-permute-start.4 = (f32[1,1,128]{2,1,0:T(1,128)S(1)}, f32[1,1,128]{2,1,0:T(1,128)S(1)}, u32[]{:S(2)}, u32[]{:S(2)}) collective-permute-start(f32[1,1,128]{2,1,0:T(1,128)S(1)} %get-tuple-element.77), channel_id=1, source_target_pairs={{0,4},{4,8},{8,12},{1,5},{5,9},{9,13},{2,6},{6,10},{10,14},{3,7},{... | collective-permute-start | bytes 1544 | tf_op jit(solution)/shard_map/ppermute | solution.py:19
  54.9 5.0 %collective-permute-start.5 = (f32[1,1,128]{2,1,0:T(1,128)S(1)}, f32[1,1,128]{2,1,0:T(1,128)S(1)}, u32[]{:S(2)}, u32[]{:S(2)}) collective-permute-start(f32[1,1,128]{2,1,0:T(1,128)S(1)} %get-tuple-element.78), channel_id=1, source_target_pairs={{4,0},{8,4},{12,8},{5,1},{9,5},{13,9},{6,2},{10,6},{14,10},{7,3},{... | collective-permute-start | bytes 1544 | tf_op jit(solution)/shard_map/ppermute | solution.py:21
  60.0 7.5 %collective-permute-start.6 = (f32[1,18,1]{2,1,0:T(8,128)S(1)}, f32[1,18,1]{2,1,0:T(8,128)S(1)}, u32[]{:S(2)}, u32[]{:S(2)}) collective-permute-start(f32[1,18,1]{2,1,0:T(8,128)S(1)} %get-tuple-element.67), channel_id=1, source_target_pairs={{0,1},{1,2},{2,3},{3,0},{4,5},{5,6},{6,7},{7,4},{8,9},{9,10},{10,1... | collective-permute-start | bytes 224 | tf_op jit(solution)/shard_map/ppermute | solution.py:19
  60.8 5.8 %collective-permute-start.2 = (f32[2,18,1]{2,1,0:T(8,128)S(1)}, f32[2,18,1]{2,1,0:T(8,128)S(1)}, u32[]{:S(2)}, u32[]{:S(2)}) collective-permute-start(f32[2,18,1]{2,1,0:T(8,128)S(1)} %get-tuple-element.55), channel_id=1, source_target_pairs={{0,1},{1,2},{2,3},{3,0},{4,5},{5,6},{6,7},{7,4},{8,9},{9,10},{10,1... | collective-permute-start | bytes 440 | tf_op jit(solution)/shard_map/ppermute | solution.py:19
  61.0 5.7 %collective-permute-start.3 = (f32[2,18,1]{2,1,0:T(8,128)S(1)}, f32[2,18,1]{2,1,0:T(8,128)S(1)}, u32[]{:S(2)}, u32[]{:S(2)}) collective-permute-start(f32[2,18,1]{2,1,0:T(8,128)S(1)} %get-tuple-element.56), channel_id=1, source_target_pairs={{1,0},{2,1},{3,2},{0,3},{5,4},{6,5},{7,6},{4,7},{9,8},{10,9},{11,1... | collective-permute-start | bytes 440 | tf_op jit(solution)/shard_map/ppermute | solution.py:21
  72.3 6.0 %collective-permute-start.9 = (f32[1,1,128]{2,1,0:T(1,128)S(1)}, f32[1,1,128]{2,1,0:T(1,128)S(1)}, u32[]{:S(2)}, u32[]{:S(2)}) collective-permute-start(f32[1,1,128]{2,1,0:T(1,128)S(1)} %get-tuple-element.76), channel_id=1, source_target_pairs={{4,0},{8,4},{12,8},{5,1},{9,5},{13,9},{6,2},{10,6},{14,10},{7,3},{... | collective-permute-start | bytes 1544 | tf_op jit(solution)/shard_map/ppermute | solution.py:21
  78.4 5.5 %collective-permute-start.10 = (f32[1,18,1]{2,1,0:T(8,128)S(1)}, f32[1,18,1]{2,1,0:T(8,128)S(1)}, u32[]{:S(2)}, u32[]{:S(2)}) collective-permute-start(f32[1,18,1]{2,1,0:T(8,128)S(1)} %get-tuple-element.65), channel_id=1, source_target_pairs={{0,1},{1,2},{2,3},{3,0},{4,5},{5,6},{6,7},{7,4},{8,9},{9,10},{10,1... | collective-permute-start | bytes 224 | tf_op jit(solution)/shard_map/ppermute | solution.py:19
  78.4 5.5 %collective-permute-start.11 = (f32[1,18,1]{2,1,0:T(8,128)S(1)}, f32[1,18,1]{2,1,0:T(8,128)S(1)}, u32[]{:S(2)}, u32[]{:S(2)}) collective-permute-start(f32[1,18,1]{2,1,0:T(8,128)S(1)} %get-tuple-element.66), channel_id=1, source_target_pairs={{1,0},{2,1},{3,2},{0,3},{5,4},{6,5},{7,6},{4,7},{9,8},{10,9},{11,1... | collective-permute-start | bytes 224 | tf_op jit(solution)/shard_map/ppermute | solution.py:21
  85.2 4.6 %collective-permute-start.12 = (f32[1,1,128]{2,1,0:T(1,128)S(1)}, f32[1,1,128]{2,1,0:T(1,128)S(1)}, u32[]{:S(2)}, u32[]{:S(2)}) collective-permute-start(f32[1,1,128]{2,1,0:T(1,128)S(1)} %get-tuple-element.73), channel_id=1, source_target_pairs={{0,4},{4,8},{8,12},{1,5},{5,9},{9,13},{2,6},{6,10},{10,14},{3,7},{... | collective-permute-start | bytes 1544 | tf_op jit(solution)/shard_map/ppermute | solution.py:19
  92.2 5.5 %collective-permute-start.14 = (f32[1,18,1]{2,1,0:T(8,128)S(1)}, f32[1,18,1]{2,1,0:T(8,128)S(1)}, u32[]{:S(2)}, u32[]{:S(2)}) collective-permute-start(f32[1,18,1]{2,1,0:T(8,128)S(1)} %get-tuple-element.63), channel_id=1, source_target_pairs={{0,1},{1,2},{2,3},{3,0},{4,5},{5,6},{6,7},{7,4},{8,9},{9,10},{10,1... | collective-permute-start | bytes 224 | tf_op jit(solution)/shard_map/ppermute | solution.py:19
  99.0 4.7 %collective-permute-start.16 = (f32[1,1,128]{2,1,0:T(1,128)S(1)}, f32[1,1,128]{2,1,0:T(1,128)S(1)}, u32[]{:S(2)}, u32[]{:S(2)}) collective-permute-start(f32[1,1,128]{2,1,0:T(1,128)S(1)} %get-tuple-element.71), channel_id=1, source_target_pairs={{0,4},{4,8},{8,12},{1,5},{5,9},{9,13},{2,6},{6,10},{10,14},{3,7},{... | collective-permute-start | bytes 1544 | tf_op jit(solution)/shard_map/ppermute | solution.py:19
  106.0 5.5 %collective-permute-start.18 = (f32[1,18,1]{2,1,0:T(8,128)S(1)}, f32[1,18,1]{2,1,0:T(8,128)S(1)}, u32[]{:S(2)}, u32[]{:S(2)}) collective-permute-start(f32[1,18,1]{2,1,0:T(8,128)S(1)} %get-tuple-element.61), channel_id=1, source_target_pairs={{0,1},{1,2},{2,3},{3,0},{4,5},{5,6},{6,7},{7,4},{8,9},{9,10},{10,1... | collective-permute-start | bytes 224 | tf_op jit(solution)/shard_map/ppermute | solution.py:19
  112.8 9.5 %collective-permute-start.20 = (f32[1,1,128]{2,1,0:T(1,128)S(1)}, f32[1,1,128]{2,1,0:T(1,128)S(1)}, u32[]{:S(2)}, u32[]{:S(2)}) collective-permute-start(f32[1,1,128]{2,1,0:T(1,128)S(1)} %get-tuple-element.69), channel_id=1, source_target_pairs={{0,4},{4,8},{8,12},{1,5},{5,9},{9,13},{2,6},{6,10},{10,14},{3,7},{... | collective-permute-start | bytes 1544 | tf_op jit(solution)/shard_map/ppermute | solution.py:19
  116.2 6.1 %collective-permute-start.21 = (f32[1,1,128]{2,1,0:T(1,128)S(1)}, f32[1,1,128]{2,1,0:T(1,128)S(1)}, u32[]{:S(2)}, u32[]{:S(2)}) collective-permute-start(f32[1,1,128]{2,1,0:T(1,128)S(1)} %get-tuple-element.70), channel_id=1, source_target_pairs={{4,0},{8,4},{12,8},{5,1},{9,5},{13,9},{6,2},{10,6},{14,10},{7,3},{... | collective-permute-start | bytes 1544 | tf_op jit(solution)/shard_map/ppermute | solution.py:21
  117.5 14.9 %collective-permute-start.24 = (bf16[1,1,128,128]{3,2,1,0:T(8,128)(2,1)S(1)}, bf16[1,1,128,128]{3,2,1,0:T(8,128)(2,1)S(1)}, u32[]{:S(2)}, u32[]{:S(2)}) collective-permute-start(bf16[1,1,128,128]{3,2,1,0:T(8,128)(2,1)S(1)} %get-tuple-element.52), channel_id=1, source_target_pairs={{0,4},{4,8},{8,12},{1,5},{5,9},{9,13},{2,6},{6,10},{10,14},{3,7},{... | collective-permute-start | bytes 98312 | tf_op jit(solution)/shard_map/ppermute | solution.py:19
  121.0 11.5 %collective-permute-start.25 = (bf16[1,1,128,128]{3,2,1,0:T(8,128)(2,1)S(1)}, bf16[1,1,128,128]{3,2,1,0:T(8,128)(2,1)S(1)}, u32[]{:S(2)}, u32[]{:S(2)}) collective-permute-start(bf16[1,1,128,128]{3,2,1,0:T(8,128)(2,1)S(1)} %get-tuple-element.51), channel_id=1, source_target_pairs={{4,0},{8,4},{12,8},{5,1},{9,5},{13,9},{6,2},{10,6},{14,10},{7,3},{... | collective-permute-start | bytes 98312 | tf_op jit(solution)/shard_map/ppermute | solution.py:21
  122.4 5.5 %collective-permute-start.22 = (f32[1,18,1]{2,1,0:T(8,128)S(1)}, f32[1,18,1]{2,1,0:T(8,128)S(1)}, u32[]{:S(2)}, u32[]{:S(2)}) collective-permute-start(f32[1,18,1]{2,1,0:T(8,128)S(1)} %get-tuple-element.59), channel_id=1, source_target_pairs={{0,1},{1,2},{2,3},{3,0},{4,5},{5,6},{6,7},{7,4},{8,9},{9,10},{10,1... | collective-permute-start | bytes 224 | tf_op jit(solution)/shard_map/ppermute | solution.py:19
  132.9 5.6 %collective-permute-start.26 = (bf16[1,18,1,128]{3,2,1,0:T(2,128)(2,1)S(1)}, bf16[1,18,1,128]{3,2,1,0:T(2,128)(2,1)S(1)}, u32[]{:S(2)}, u32[]{:S(2)}) collective-permute-start(bf16[1,18,1,128]{3,2,1,0:T(2,128)(2,1)S(1)} %get-tuple-element.42), channel_id=1, source_target_pairs={{0,1},{1,2},{2,3},{3,0},{4,5},{5,6},{6,7},{7,4},{8,9},{9,10},{10,1... | collective-permute-start | bytes 13832 | tf_op jit(solution)/shard_map/ppermute | solution.py:19
  146.9 49.1 %collective-permute-start.28 = (bf16[1,1,128,128]{3,2,1,0:T(8,128)(2,1)S(1)}, bf16[1,1,128,128]{3,2,1,0:T(8,128)(2,1)S(1)}, u32[]{:S(2)}, u32[]{:S(2)}) collective-permute-start(bf16[1,1,128,128]{3,2,1,0:T(8,128)(2,1)S(1)} %get-tuple-element.46), channel_id=1, source_target_pairs={{0,4},{4,8},{8,12},{1,5},{5,9},{9,13},{2,6},{6,10},{10,14},{3,7},{... | collective-permute-start | bytes 98312 | tf_op jit(solution)/shard_map/ppermute | solution.py:19
  149.1 46.9 %collective-permute-start.29 = (bf16[1,1,128,128]{3,2,1,0:T(8,128)(2,1)S(1)}, bf16[1,1,128,128]{3,2,1,0:T(8,128)(2,1)S(1)}, u32[]{:S(2)}, u32[]{:S(2)}) collective-permute-start(bf16[1,1,128,128]{3,2,1,0:T(8,128)(2,1)S(1)} %get-tuple-element.47), channel_id=1, source_target_pairs={{4,0},{8,4},{12,8},{5,1},{9,5},{13,9},{6,2},{10,6},{14,10},{7,3},{... | collective-permute-start | bytes 98312 | tf_op jit(solution)/shard_map/ppermute | solution.py:21
  198.3 5.5 %collective-permute-start.31 = (bf16[1,18,1,128]{3,2,1,0:T(2,128)(2,1)S(1)}, bf16[1,18,1,128]{3,2,1,0:T(2,128)(2,1)S(1)}, u32[]{:S(2)}, u32[]{:S(2)}) collective-permute-start(bf16[1,18,1,128]{3,2,1,0:T(2,128)(2,1)S(1)} %get-tuple-element.38), channel_id=1, source_target_pairs={{0,1},{1,2},{2,3},{3,0},{4,5},{5,6},{6,7},{7,4},{8,9},{9,10},{10,1... | collective-permute-start | bytes 13832 | tf_op jit(solution)/shard_map/ppermute | solution.py:19
  (15 other events, 273.1 us)
Sparse Core Ops, SparseCore 0:
  147.0 57.9 reduce-scatter.1
where the time goes:
time: 227 us; the launch traced here: 225 us
  blocking collectives  91.5 us (40%)
  starting transfers between devices  60.1 us (26%)
  waiting for transfers between devices  23.7 us (10%)
  other arithmetic  18.9 us (8%)
  between operations  15.9 us (7%)
  matrix products  9.55 us (4%)
  local copies, waits for them, and re-layouts  5.66 us (2%)
    psum x1, blocking collectives, shards(): lax.psum((local_bias, local_proj), ('dp', 'lat', 'lon'))  45 us
    psum x1, blocking collectives, shards(): lax.psum((jnp.sum(mask_float), jnp.sum(mask_float * surface_cotangent, ax...  36.6 us
    ppermute x16, starting transfers between devices, extended(): lax.ppermute(head, axis, [((i + 1) % count, i) for i in range(ends)])  32.9 us
    ppermute x16, starting transfers between devices, extended(): lax.ppermute(tail, axis, [(i, (i + 1) % count) for i in range(ends)])  27.1 us
    ppermute x16, waiting for transfers between devices, extended(): lax.ppermute(tail, axis, [(i, (i + 1) % count) for i in range(ends)])  11.9 us
    ppermute x16, waiting for transfers between devices, extended(): lax.ppermute(head, axis, [((i + 1) % count, i) for i in range(ends)])  11.7 us
    psum x1, blocking collectives, shards(): own_weight = lax.psum(spatial, 'dp')  9.87 us
    add x4, other arithmetic, solve_steps(): direction = residual + step_beta[turn_index] * direction  5.32 us
  transfers between devices with their start and end apart: 33, of which 12 were waited for; matrix products, arithmetic and copies ran while one was open for 8% of the time, Pallas kernels for 0%

commit v1 on v0

--- a/solution.py
+++ b/solution.py
@@ -137,7 +137,7 @@
         tiled=True,
     )
     own_weight = lax.psum(spatial, "dp")
-    total_bias, total_proj = lax.psum((local_bias, local_proj), ("dp", "lat", "lon"))
+    total_bias, total_proj = lax.psum(lax.psum((local_bias, local_proj), "dp"), ("lat", "lon"))
     all_cells = cell_count * lax.axis_size("dp") * lax.axis_size("lat") * lax.axis_size("lon")
     grad_scale = 1.0 / math.sqrt(all_cells)
     return (grad_hidden, own_weight * grad_scale, total_bias * grad_scale, total_proj * grad_scale)

time: 227 us -> 260 us (1.15)
  waiting for transfers between devices: 23.7 us -> 70.4 us
  blocking collectives: 91.5 us -> 76.7 us
    reduce_scatter x1, waiting for transfers between devices: 0.01 us -> 42.9 us  [shards(): lax.psum_scatter(jnp.stack(blocks, axis=1).reshape(share * lax.axis_size(...]
    psum x1, blocking collectives: 45 us -> 31.1 us  [shards(): lax.psum(lax.psum((local_bias, local_proj), 'dp'), ('lat', 'lon'))]
    ppermute x16, waiting for transfers between devices: 11.7 us -> 15.6 us  [extended(): lax.ppermute(head, axis, [((i + 1) % count, i) for i in range(ends)])]
  transfers between devices with their start and end apart: 33 -> 33, of which waited for: 12 -> 14; matrix products, arithmetic and copies ran while one was open for 8% -> 7% of each run, Pallas kernels for 0% -> 0%
where the time goes in v1:
time: 260 us; the launch traced here: 259 us
  blocking collectives  76.7 us (30%)
  waiting for transfers between devices  70.4 us (27%)
  starting transfers between devices  61.7 us (24%)
  other arithmetic  19 us (7%)
  between operations  15.9 us (6%)
  matrix products  9.55 us (4%)
  local copies, waits for them, and re-layouts  5.76 us (2%)
    reduce_scatter x1, waiting for transfers between devices, shards(): lax.psum_scatter(jnp.stack(blocks, axis=1).reshape(share * lax.axis_size(...  42.9 us
    psum x1, blocking collectives, shards(): lax.psum((jnp.sum(mask_float), jnp.sum(mask_float * surface_cotangent, ax...  36.6 us
    ppermute x16, starting transfers between devices, extended(): lax.ppermute(head, axis, [((i + 1) % count, i) for i in range(ends)])  34.4 us
    psum x1, blocking collectives, shards(): lax.psum(lax.psum((local_bias, local_proj), 'dp'), ('lat', 'lon'))  31.1 us
    ppermute x16, starting transfers between devices, extended(): lax.ppermute(tail, axis, [(i, (i + 1) % count) for i in range(ends)])  27.2 us
    ppermute x16, waiting for transfers between devices, extended(): lax.ppermute(head, axis, [((i + 1) % count, i) for i in range(ends)])  15.6 us
    ppermute x16, waiting for transfers between devices, extended(): lax.ppermute(tail, axis, [(i, (i + 1) % count) for i in range(ends)])  11.9 us
    psum x1, blocking collectives, shards(): own_weight = lax.psum(spatial, 'dp')  9.03 us
  transfers between devices with their start and end apart: 33, of which 14 were waited for; matrix products, arithmetic and copies ran while one was open for 7% of the time, Pallas kernels for 0%

profile of v1, /device:TPU:0, one launch (start us, length us, event | category | flops | bytes accessed | tf_op | source)
XLA Modules:
  0.0 259.0 jit_solution(6203430556448238331)
XLA Ops:
  8.7 2.4 collective-permute-start
  15.0 36.6 %all-reduce.1 = (f32[1]{0:T(128)}, f32[1]{0:T(128)}) all-reduce(f32[1]{0:T(128)} %bitcast.2, f32[1]{0:T(128)} %bitcast.3), channel_id=1, replica_groups=mesh['dp'=2,'lat'=4,'lon'=4] {'lat','lon'}, use_global_device_ids=true, to_apply=%region_1.0 | all-reduce | flops 2 | bytes 16 | tf_op jit(solution)/shard_map/psum | solution.py:75
  61.0 3.7 %collective-permute-start.3 = (f32[2,18,1]{2,1,0:T(8,128)S(1)}, f32[2,18,1]{2,1,0:T(8,128)S(1)}, u32[]{:S(2)}, u32[]{:S(2)}) collective-permute-start(f32[2,18,1]{2,1,0:T(8,128)S(1)} %get-tuple-element.59), channel_id=1, source_target_pairs={{1,0},{2,1},{3,2},{0,3},{5,4},{6,5},{7,6},{4,7},{9,8},{10,9},{11,1... | collective-permute-start | bytes 440 | tf_op jit(solution)/shard_map/ppermute | solution.py:21
  69.8 2.6 %collective-permute-start.8 = (f32[1,1,128]{2,1,0:T(1,128)S(1)}, f32[1,1,128]{2,1,0:T(1,128)S(1)}, u32[]{:S(2)}, u32[]{:S(2)}) collective-permute-start(f32[1,1,128]{2,1,0:T(1,128)S(1)} %get-tuple-element.78), channel_id=1, source_target_pairs={{0,4},{4,8},{8,12},{1,5},{5,9},{9,13},{2,6},{6,10},{10,14},{3,7},{... | collective-permute-start | bytes 1544 | tf_op jit(solution)/shard_map/ppermute | solution.py:19
  73.8 4.7 %collective-permute-done.9 = f32[1,1,128]{2,1,0:T(1,128)S(1)} collective-permute-done((f32[1,1,128]{2,1,0:T(1,128)S(1)}, f32[1,1,128]{2,1,0:T(1,128)S(1)}, u32[]{:S(2)}, u32[]{:S(2)}) %collective-permute-start.9) | collective-permute-done | bytes 544 | tf_op jit(solution)/shard_map/ppermute | solution.py:21
  78.6 3.8 %collective-permute-start.11 = (f32[1,18,1]{2,1,0:T(8,128)S(1)}, f32[1,18,1]{2,1,0:T(8,128)S(1)}, u32[]{:S(2)}, u32[]{:S(2)}) collective-permute-start(f32[1,18,1]{2,1,0:T(8,128)S(1)} %get-tuple-element.69), channel_id=1, source_target_pairs={{1,0},{2,1},{3,2},{0,3},{5,4},{6,5},{7,6},{4,7},{9,8},{10,9},{11,1... | collective-permute-start | bytes 224 | tf_op jit(solution)/shard_map/ppermute | solution.py:21
  85.3 3.3 %collective-permute-start.12 = (f32[1,1,128]{2,1,0:T(1,128)S(1)}, f32[1,1,128]{2,1,0:T(1,128)S(1)}, u32[]{:S(2)}, u32[]{:S(2)}) collective-permute-start(f32[1,1,128]{2,1,0:T(1,128)S(1)} %get-tuple-element.76), channel_id=1, source_target_pairs={{0,4},{4,8},{8,12},{1,5},{5,9},{9,13},{2,6},{6,10},{10,14},{3,7},{... | collective-permute-start | bytes 1544 | tf_op jit(solution)/shard_map/ppermute | solution.py:19
  90.0 2.2 collective-permute-done.13
  93.3 2.8 %collective-permute-start.15 = (f32[1,18,1]{2,1,0:T(8,128)S(1)}, f32[1,18,1]{2,1,0:T(8,128)S(1)}, u32[]{:S(2)}, u32[]{:S(2)}) collective-permute-start(f32[1,18,1]{2,1,0:T(8,128)S(1)} %get-tuple-element.67), channel_id=1, source_target_pairs={{1,0},{2,1},{3,2},{0,3},{5,4},{6,5},{7,6},{4,7},{9,8},{10,9},{11,1... | collective-permute-start | bytes 224 | tf_op jit(solution)/shard_map/ppermute | solution.py:21
  99.1 3.4 %collective-permute-start.16 = (f32[1,1,128]{2,1,0:T(1,128)S(1)}, f32[1,1,128]{2,1,0:T(1,128)S(1)}, u32[]{:S(2)}, u32[]{:S(2)}) collective-permute-start(f32[1,1,128]{2,1,0:T(1,128)S(1)} %get-tuple-element.74), channel_id=1, source_target_pairs={{0,4},{4,8},{8,12},{1,5},{5,9},{9,13},{2,6},{6,10},{10,14},{3,7},{... | collective-permute-start | bytes 1544 | tf_op jit(solution)/shard_map/ppermute | solution.py:19
  103.8 2.2 collective-permute-done.17
  107.3 2.6 %collective-permute-start.19 = (f32[1,18,1]{2,1,0:T(8,128)S(1)}, f32[1,18,1]{2,1,0:T(8,128)S(1)}, u32[]{:S(2)}, u32[]{:S(2)}) collective-permute-start(f32[1,18,1]{2,1,0:T(8,128)S(1)} %get-tuple-element.65), channel_id=1, source_target_pairs={{1,0},{2,1},{3,2},{0,3},{5,4},{6,5},{7,6},{4,7},{9,8},{10,9},{11,1... | collective-permute-start | bytes 224 | tf_op jit(solution)/shard_map/ppermute | solution.py:21
  113.0 3.4 %collective-permute-start.20 = (f32[1,1,128]{2,1,0:T(1,128)S(1)}, f32[1,1,128]{2,1,0:T(1,128)S(1)}, u32[]{:S(2)}, u32[]{:S(2)}) collective-permute-start(f32[1,1,128]{2,1,0:T(1,128)S(1)} %get-tuple-element.72), channel_id=1, source_target_pairs={{0,4},{4,8},{8,12},{1,5},{5,9},{9,13},{2,6},{6,10},{10,14},{3,7},{... | collective-permute-start | bytes 1544 | tf_op jit(solution)/shard_map/ppermute | solution.py:19
  117.7 3.5 %collective-permute-start.24 = (bf16[1,1,128,128]{3,2,1,0:T(8,128)(2,1)S(1)}, bf16[1,1,128,128]{3,2,1,0:T(8,128)(2,1)S(1)}, u32[]{:S(2)}, u32[]{:S(2)}) collective-permute-start(bf16[1,1,128,128]{3,2,1,0:T(8,128)(2,1)S(1)} %get-tuple-element.55), channel_id=1, source_target_pairs={{0,4},{4,8},{8,12},{1,5},{5,9},{9,13},{2,6},{6,10},{10,14},{3,7},{... | collective-permute-start | bytes 98312 | tf_op jit(solution)/shard_map/ppermute | solution.py:19
  123.9 2.6 %collective-permute-start.23 = (f32[1,18,1]{2,1,0:T(8,128)S(1)}, f32[1,18,1]{2,1,0:T(8,128)S(1)}, u32[]{:S(2)}, u32[]{:S(2)}) collective-permute-start(f32[1,18,1]{2,1,0:T(8,128)S(1)} %get-tuple-element.63), channel_id=1, source_target_pairs={{1,0},{2,1},{3,2},{0,3},{5,4},{6,5},{7,6},{4,7},{9,8},{10,9},{11,1... | collective-permute-start | bytes 224 | tf_op jit(solution)/shard_map/ppermute | solution.py:21
  128.1 4.4 %fusion.69 = f32[2048]{0:T(1024)S(1)} fusion(f32[1,16,128]{2,1,0:T(8,128)S(1)} %get-tuple-element.14, f32[1,16,128]{2,1,0:T(8,128)S(1)} %get-tuple-element.24, f32[1,16,128]{2,1,0:T(8,128)S(1)} %get-tuple-element.13, f32[1,18,1]{2,1,0:T(8,128)S(1)} %collective-permute-done.23, f32[1,1,128]{2,1,0:T(1,128)S(1)} %collective-permute-done.21, ...), kind=kLoop, calls=%fused_computation.128 | loop fusion | flops 79872 | bytes 107692 | tf_op jit(solution)/shard_map/mul | solution.py:105
  134.3 2.6 %collective-permute-start.27 = (bf16[1,18,1,128]{3,2,1,0:T(2,128)(2,1)S(1)}, bf16[1,18,1,128]{3,2,1,0:T(2,128)(2,1)S(1)}, u32[]{:S(2)}, u32[]{:S(2)}) collective-permute-start(bf16[1,18,1,128]{3,2,1,0:T(2,128)(2,1)S(1)} %get-tuple-element.46), channel_id=1, source_target_pairs={{1,0},{2,1},{3,2},{0,3},{5,4},{6,5},{7,6},{4,7},{9,8},{10,9},{11,1... | collective-permute-start | bytes 13832 | tf_op jit(solution)/shard_map/ppermute | solution.py:21
  145.8 2.2 collective-permute-start.28
  150.5 3.9 %collective-permute-done.29 = bf16[1,1,128,128]{3,2,1,0:T(8,128)(2,1)S(1)} collective-permute-done((bf16[1,1,128,128]{3,2,1,0:T(8,128)(2,1)S(1)}, bf16[1,1,128,128]{3,2,1,0:T(8,128)(2,1)S(1)}, u32[]{:S(2)}, u32[]{:S(2)}) %collective-permute-start.29) | collective-permute-done | bytes 32800 | tf_op jit(solution)/shard_map/ppermute | solution.py:21
  154.4 3.9 %collective-permute-start.30 = (bf16[1,18,1,128]{3,2,1,0:T(2,128)(2,1)S(1)}, bf16[1,18,1,128]{3,2,1,0:T(2,128)(2,1)S(1)}, u32[]{:S(2)}, u32[]{:S(2)}) collective-permute-start(bf16[1,18,1,128]{3,2,1,0:T(2,128)(2,1)S(1)} %get-tuple-element.40), channel_id=1, source_target_pairs={{1,0},{2,1},{3,2},{0,3},{5,4},{6,5},{7,6},{4,7},{9,8},{10,9},{11,1... | collective-permute-start | bytes 13832 | tf_op jit(solution)/shard_map/ppermute | solution.py:21
  159.7 4.1 %collective-permute-done.31 = bf16[1,18,1,128]{3,2,1,0:T(2,128)(2,1)S(1)} collective-permute-done((bf16[1,18,1,128]{3,2,1,0:T(2,128)(2,1)S(1)}, bf16[1,18,1,128]{3,2,1,0:T(2,128)(2,1)S(1)}, u32[]{:S(2)}, u32[]{:S(2)}) %collective-permute-start.31) | collective-permute-done | bytes 4640 | tf_op jit(solution)/shard_map/ppermute | solution.py:19
  168.0 42.9 %reduce-scatter.2.cloned.1.call-done = f32[8,3,3,128]{3,0,2,1:T(8,128)} async-done(((f32[128,3,3,128]{3,0,2,1:T(8,128)}), f32[8,3,3,128]{3,0,2,1:T(8,128)}) %reduce-scatter.2.cloned.1.call-update) | async-done | bytes 36880 | tf_op jit(solution)/shard_map/reduce_scatter | solution.py:133
  210.8 9.0 %all-reduce.2 = (f32[8,3,3,128]{3,0,2,1:T(8,128)S(1)}, f32[128]{0:T(128)S(1)}, f32[128]{0:T(128)S(1)}) all-reduce(f32[8,3,3,128]{3,0,2,1:T(8,128)} %reduce-scatter.2.cloned.1.call-done, f32[128]{0:T(128)S(1)} %get-tuple-element.11, f32[128]{0:T(128)S(1)} %get-tuple-element.25), channel_id=1, replica_groups=mesh['dp'=2,'lat'=4,'lon'=4] {'dp'}, use_global_device_ids=true, to_apply=%region_5.0 | all-reduce | flops 9472 | bytes 75776 | tf_op jit(solution)/shard_map/psum | solution.py:139
  220.5 31.1 %all-reduce = (f32[128]{0:T(128)S(1)}, f32[128]{0:T(128)S(1)}) all-reduce(f32[128]{0:T(128)S(1)} %get-tuple-element.9, f32[128]{0:T(128)S(1)} %get-tuple-element.10), channel_id=1, replica_groups=mesh['dp'=2,'lat'=4,'lon'=4] {'lat','lon'}, use_global_device_ids=true, to_apply=%region_8.0 | all-reduce | flops 256 | bytes 2048 | tf_op jit(solution)/shard_map/psum | solution.py:140
  (129 shorter events, 59.2 us)
Async XLA Ops:
  7.2 203.7 %reduce-scatter.2.cloned.1.call-start = ((), (), s32[]{:S(2)}) async-start(), calls=%async_computation.1 | async-start | bytes 626688 | tf_op jit(solution)/shard_map/reduce_scatter | solution.py:133
  8.7 51.3 %collective-permute-start = (f32[2,1,128]{2,1,0:T(1,128)S(1)}, f32[2,1,128]{2,1,0:T(1,128)S(1)}, u32[]{:S(2)}, u32[]{:S(2)}) collective-permute-start(f32[2,1,128]{2,1,0:T(1,128)S(1)} %get-tuple-element.60), channel_id=1, source_target_pairs={{0,4},{4,8},{8,12},{1,5},{5,9},{9,13},{2,6},{6,10},{10,14},{3,7},{... | collective-permute-start | bytes 3080 | tf_op jit(solution)/shard_map/ppermute | solution.py:19
  11.1 49.0 %collective-permute-start.1 = (f32[2,1,128]{2,1,0:T(1,128)S(1)}, f32[2,1,128]{2,1,0:T(1,128)S(1)}, u32[]{:S(2)}, u32[]{:S(2)}) collective-permute-start(f32[2,1,128]{2,1,0:T(1,128)S(1)} %get-tuple-element.61), channel_id=1, source_target_pairs={{4,0},{8,4},{12,8},{5,1},{9,5},{13,9},{6,2},{10,6},{14,10},{7,3},{... | collective-permute-start | bytes 3080 | tf_op jit(solution)/shard_map/ppermute | solution.py:21
  53.6 5.6 %collective-permute-start.4 = (f32[1,1,128]{2,1,0:T(1,128)S(1)}, f32[1,1,128]{2,1,0:T(1,128)S(1)}, u32[]{:S(2)}, u32[]{:S(2)}) collective-permute-start(f32[1,1,128]{2,1,0:T(1,128)S(1)} %get-tuple-element.80), channel_id=1, source_target_pairs={{0,4},{4,8},{8,12},{1,5},{5,9},{9,13},{2,6},{6,10},{10,14},{3,7},{... | collective-permute-start | bytes 1544 | tf_op jit(solution)/shard_map/ppermute | solution.py:19
  54.9 5.0 %collective-permute-start.5 = (f32[1,1,128]{2,1,0:T(1,128)S(1)}, f32[1,1,128]{2,1,0:T(1,128)S(1)}, u32[]{:S(2)}, u32[]{:S(2)}) collective-permute-start(f32[1,1,128]{2,1,0:T(1,128)S(1)} %get-tuple-element.81), channel_id=1, source_target_pairs={{4,0},{8,4},{12,8},{5,1},{9,5},{13,9},{6,2},{10,6},{14,10},{7,3},{... | collective-permute-start | bytes 1544 | tf_op jit(solution)/shard_map/ppermute | solution.py:21
  60.0 7.5 %collective-permute-start.6 = (f32[1,18,1]{2,1,0:T(8,128)S(1)}, f32[1,18,1]{2,1,0:T(8,128)S(1)}, u32[]{:S(2)}, u32[]{:S(2)}) collective-permute-start(f32[1,18,1]{2,1,0:T(8,128)S(1)} %get-tuple-element.70), channel_id=1, source_target_pairs={{0,1},{1,2},{2,3},{3,0},{4,5},{5,6},{6,7},{7,4},{8,9},{9,10},{10,1... | collective-permute-start | bytes 224 | tf_op jit(solution)/shard_map/ppermute | solution.py:19
  60.8 5.8 %collective-permute-start.2 = (f32[2,18,1]{2,1,0:T(8,128)S(1)}, f32[2,18,1]{2,1,0:T(8,128)S(1)}, u32[]{:S(2)}, u32[]{:S(2)}) collective-permute-start(f32[2,18,1]{2,1,0:T(8,128)S(1)} %get-tuple-element.58), channel_id=1, source_target_pairs={{0,1},{1,2},{2,3},{3,0},{4,5},{5,6},{6,7},{7,4},{8,9},{9,10},{10,1... | collective-permute-start | bytes 440 | tf_op jit(solution)/shard_map/ppermute | solution.py:19
  61.0 5.7 %collective-permute-start.3 = (f32[2,18,1]{2,1,0:T(8,128)S(1)}, f32[2,18,1]{2,1,0:T(8,128)S(1)}, u32[]{:S(2)}, u32[]{:S(2)}) collective-permute-start(f32[2,18,1]{2,1,0:T(8,128)S(1)} %get-tuple-element.59), channel_id=1, source_target_pairs={{1,0},{2,1},{3,2},{0,3},{5,4},{6,5},{7,6},{4,7},{9,8},{10,9},{11,1... | collective-permute-start | bytes 440 | tf_op jit(solution)/shard_map/ppermute | solution.py:21
  72.4 6.0 %collective-permute-start.9 = (f32[1,1,128]{2,1,0:T(1,128)S(1)}, f32[1,1,128]{2,1,0:T(1,128)S(1)}, u32[]{:S(2)}, u32[]{:S(2)}) collective-permute-start(f32[1,1,128]{2,1,0:T(1,128)S(1)} %get-tuple-element.79), channel_id=1, source_target_pairs={{4,0},{8,4},{12,8},{5,1},{9,5},{13,9},{6,2},{10,6},{14,10},{7,3},{... | collective-permute-start | bytes 1544 | tf_op jit(solution)/shard_map/ppermute | solution.py:21
  78.5 5.5 %collective-permute-start.10 = (f32[1,18,1]{2,1,0:T(8,128)S(1)}, f32[1,18,1]{2,1,0:T(8,128)S(1)}, u32[]{:S(2)}, u32[]{:S(2)}) collective-permute-start(f32[1,18,1]{2,1,0:T(8,128)S(1)} %get-tuple-element.68), channel_id=1, source_target_pairs={{0,1},{1,2},{2,3},{3,0},{4,5},{5,6},{6,7},{7,4},{8,9},{9,10},{10,1... | collective-permute-start | bytes 224 | tf_op jit(solution)/shard_map/ppermute | solution.py:19
  78.6 5.5 %collective-permute-start.11 = (f32[1,18,1]{2,1,0:T(8,128)S(1)}, f32[1,18,1]{2,1,0:T(8,128)S(1)}, u32[]{:S(2)}, u32[]{:S(2)}) collective-permute-start(f32[1,18,1]{2,1,0:T(8,128)S(1)} %get-tuple-element.69), channel_id=1, source_target_pairs={{1,0},{2,1},{3,2},{0,3},{5,4},{6,5},{7,6},{4,7},{9,8},{10,9},{11,1... | collective-permute-start | bytes 224 | tf_op jit(solution)/shard_map/ppermute | solution.py:21
  92.3 5.5 %collective-permute-start.14 = (f32[1,18,1]{2,1,0:T(8,128)S(1)}, f32[1,18,1]{2,1,0:T(8,128)S(1)}, u32[]{:S(2)}, u32[]{:S(2)}) collective-permute-start(f32[1,18,1]{2,1,0:T(8,128)S(1)} %get-tuple-element.66), channel_id=1, source_target_pairs={{0,1},{1,2},{2,3},{3,0},{4,5},{5,6},{6,7},{7,4},{8,9},{9,10},{10,1... | collective-permute-start | bytes 224 | tf_op jit(solution)/shard_map/ppermute | solution.py:19
  99.1 4.7 %collective-permute-start.16 = (f32[1,1,128]{2,1,0:T(1,128)S(1)}, f32[1,1,128]{2,1,0:T(1,128)S(1)}, u32[]{:S(2)}, u32[]{:S(2)}) collective-permute-start(f32[1,1,128]{2,1,0:T(1,128)S(1)} %get-tuple-element.74), channel_id=1, source_target_pairs={{0,4},{4,8},{8,12},{1,5},{5,9},{9,13},{2,6},{6,10},{10,14},{3,7},{... | collective-permute-start | bytes 1544 | tf_op jit(solution)/shard_map/ppermute | solution.py:19
  106.1 5.5 %collective-permute-start.18 = (f32[1,18,1]{2,1,0:T(8,128)S(1)}, f32[1,18,1]{2,1,0:T(8,128)S(1)}, u32[]{:S(2)}, u32[]{:S(2)}) collective-permute-start(f32[1,18,1]{2,1,0:T(8,128)S(1)} %get-tuple-element.64), channel_id=1, source_target_pairs={{0,1},{1,2},{2,3},{3,0},{4,5},{5,6},{6,7},{7,4},{8,9},{9,10},{10,1... | collective-permute-start | bytes 224 | tf_op jit(solution)/shard_map/ppermute | solution.py:19
  113.0 9.5 %collective-permute-start.20 = (f32[1,1,128]{2,1,0:T(1,128)S(1)}, f32[1,1,128]{2,1,0:T(1,128)S(1)}, u32[]{:S(2)}, u32[]{:S(2)}) collective-permute-start(f32[1,1,128]{2,1,0:T(1,128)S(1)} %get-tuple-element.72), channel_id=1, source_target_pairs={{0,4},{4,8},{8,12},{1,5},{5,9},{9,13},{2,6},{6,10},{10,14},{3,7},{... | collective-permute-start | bytes 1544 | tf_op jit(solution)/shard_map/ppermute | solution.py:19
  116.4 6.1 %collective-permute-start.21 = (f32[1,1,128]{2,1,0:T(1,128)S(1)}, f32[1,1,128]{2,1,0:T(1,128)S(1)}, u32[]{:S(2)}, u32[]{:S(2)}) collective-permute-start(f32[1,1,128]{2,1,0:T(1,128)S(1)} %get-tuple-element.73), channel_id=1, source_target_pairs={{4,0},{8,4},{12,8},{5,1},{9,5},{13,9},{6,2},{10,6},{14,10},{7,3},{... | collective-permute-start | bytes 1544 | tf_op jit(solution)/shard_map/ppermute | solution.py:21
  117.7 14.9 %collective-permute-start.24 = (bf16[1,1,128,128]{3,2,1,0:T(8,128)(2,1)S(1)}, bf16[1,1,128,128]{3,2,1,0:T(8,128)(2,1)S(1)}, u32[]{:S(2)}, u32[]{:S(2)}) collective-permute-start(bf16[1,1,128,128]{3,2,1,0:T(8,128)(2,1)S(1)} %get-tuple-element.55), channel_id=1, source_target_pairs={{0,4},{4,8},{8,12},{1,5},{5,9},{9,13},{2,6},{6,10},{10,14},{3,7},{... | collective-permute-start | bytes 98312 | tf_op jit(solution)/shard_map/ppermute | solution.py:19
  121.2 11.4 %collective-permute-start.25 = (bf16[1,1,128,128]{3,2,1,0:T(8,128)(2,1)S(1)}, bf16[1,1,128,128]{3,2,1,0:T(8,128)(2,1)S(1)}, u32[]{:S(2)}, u32[]{:S(2)}) collective-permute-start(bf16[1,1,128,128]{3,2,1,0:T(8,128)(2,1)S(1)} %get-tuple-element.54), channel_id=1, source_target_pairs={{4,0},{8,4},{12,8},{5,1},{9,5},{13,9},{6,2},{10,6},{14,10},{7,3},{... | collective-permute-start | bytes 98312 | tf_op jit(solution)/shard_map/ppermute | solution.py:21
  122.6 5.5 %collective-permute-start.22 = (f32[1,18,1]{2,1,0:T(8,128)S(1)}, f32[1,18,1]{2,1,0:T(8,128)S(1)}, u32[]{:S(2)}, u32[]{:S(2)}) collective-permute-start(f32[1,18,1]{2,1,0:T(8,128)S(1)} %get-tuple-element.62), channel_id=1, source_target_pairs={{0,1},{1,2},{2,3},{3,0},{4,5},{5,6},{6,7},{7,4},{8,9},{9,10},{10,1... | collective-permute-start | bytes 224 | tf_op jit(solution)/shard_map/ppermute | solution.py:19
  133.0 5.6 %collective-permute-start.26 = (bf16[1,18,1,128]{3,2,1,0:T(2,128)(2,1)S(1)}, bf16[1,18,1,128]{3,2,1,0:T(2,128)(2,1)S(1)}, u32[]{:S(2)}, u32[]{:S(2)}) collective-permute-start(bf16[1,18,1,128]{3,2,1,0:T(2,128)(2,1)S(1)} %get-tuple-element.45), channel_id=1, source_target_pairs={{0,1},{1,2},{2,3},{3,0},{4,5},{5,6},{6,7},{7,4},{8,9},{9,10},{10,1... | collective-permute-start | bytes 13832 | tf_op jit(solution)/shard_map/ppermute | solution.py:19
  145.8 4.7 %collective-permute-start.28 = (bf16[1,1,128,128]{3,2,1,0:T(8,128)(2,1)S(1)}, bf16[1,1,128,128]{3,2,1,0:T(8,128)(2,1)S(1)}, u32[]{:S(2)}, u32[]{:S(2)}) collective-permute-start(bf16[1,1,128,128]{3,2,1,0:T(8,128)(2,1)S(1)} %get-tuple-element.49), channel_id=1, source_target_pairs={{0,4},{4,8},{8,12},{1,5},{5,9},{9,13},{2,6},{6,10},{10,14},{3,7},{... | collective-permute-start | bytes 98312 | tf_op jit(solution)/shard_map/ppermute | solution.py:19
  148.0 6.4 %collective-permute-start.29 = (bf16[1,1,128,128]{3,2,1,0:T(8,128)(2,1)S(1)}, bf16[1,1,128,128]{3,2,1,0:T(8,128)(2,1)S(1)}, u32[]{:S(2)}, u32[]{:S(2)}) collective-permute-start(bf16[1,1,128,128]{3,2,1,0:T(8,128)(2,1)S(1)} %get-tuple-element.50), channel_id=1, source_target_pairs={{4,0},{8,4},{12,8},{5,1},{9,5},{13,9},{6,2},{10,6},{14,10},{7,3},{... | collective-permute-start | bytes 98312 | tf_op jit(solution)/shard_map/ppermute | solution.py:21
  154.4 5.3 %collective-permute-start.30 = (bf16[1,18,1,128]{3,2,1,0:T(2,128)(2,1)S(1)}, bf16[1,18,1,128]{3,2,1,0:T(2,128)(2,1)S(1)}, u32[]{:S(2)}, u32[]{:S(2)}) collective-permute-start(bf16[1,18,1,128]{3,2,1,0:T(2,128)(2,1)S(1)} %get-tuple-element.40), channel_id=1, source_target_pairs={{1,0},{2,1},{3,2},{0,3},{5,4},{6,5},{7,6},{4,7},{9,8},{10,9},{11,1... | collective-permute-start | bytes 13832 | tf_op jit(solution)/shard_map/ppermute | solution.py:21
  158.3 5.5 %collective-permute-start.31 = (bf16[1,18,1,128]{3,2,1,0:T(2,128)(2,1)S(1)}, bf16[1,18,1,128]{3,2,1,0:T(2,128)(2,1)S(1)}, u32[]{:S(2)}, u32[]{:S(2)}) collective-permute-start(bf16[1,18,1,128]{3,2,1,0:T(2,128)(2,1)S(1)} %get-tuple-element.41), channel_id=1, source_target_pairs={{0,1},{1,2},{2,3},{3,0},{4,5},{5,6},{6,7},{7,4},{8,9},{9,10},{10,1... | collective-permute-start | bytes 13832 | tf_op jit(solution)/shard_map/ppermute | solution.py:19
  (15 other events, 274.4 us)
Sparse Core Ops, SparseCore 0:
  150.7 60.1 reduce-scatter.1
